TPU v7x, 32 devices: a whole 2x2x4 slice. The times are simulated.
32 devices in a mesh: rows: 8 (over z, y), grp: 4 (over x, core).
Axes of the slice: x: 2, y: 2, z: 4, core: 2. Of those that a mesh axis runs over, the one named last changes fastest.
Arguments:
- table: float32 [65536, 256], P(('rows', 'grp')), may hold values from -1.5 to 1.5
- hot_slot: int32 [512], P(('rows', 'grp')), may hold values from 0 to 2047, as said below
- cold_row: int32 [32, 32, 64], P(('rows', 'grp')), may hold values from 0 to 2047, as said below
- cold_bag: int32 [32, 32, 64], P(('rows', 'grp')), may hold values from 0 to 511
- hot_pick: int32 [8192, 8], P(('rows', 'grp')), may hold values from 0 to 511
- dense: float32 [8192, 256], P(('rows', 'grp')), may hold values from -6 to 6
- label: int32 [8192], P(('rows', 'grp')), may hold values 0 or 1
Outputs:
- pooled: float32 [8192, 256], P(('rows', 'grp'))
- new_table: float32 [65536, 256], P(('rows', 'grp'))
- hot_new: float32 [512, 256], replicated
Inputs may be any that keep to these rules, and one draw needn't show every extreme that they name: `hot_slot`: distinct within each device's block of 16 entries; hot row h lies in the shard of device h // 16. `cold_row`: a cold slot never names a hot row of its owner. `cold_bag`: a value of 256 or more marks an empty slot.
All inputs are finite; a program needn't handle non-finite values. No bound on the sum of `label` on one device may be relied on, other than what follows from the above.
Results may differ from a plain program's by a relative error of at most 0.0029.
Values may be sent and summed in bfloat16 or wider, within the bound.
No kernel may reach another device: no remote copies, remote signals or barrier semaphores. Data moves between devices by JAX's collectives and lax.ppermute only.
A program may use at most 64 MiB of HBM per device.

v0:
```python
import jax
import jax.numpy as jnp
from jax import lax
from jax.sharding import PartitionSpec as P


def body(table, hot_slot, cold_row, cold_bag, hot_pick, dense, label):
    n_rows = lax.axis_size("rows")
    n_grp = lax.axis_size("grp")
    width = table.shape[1]
    samples = dense.shape[0]
    own_hot = hot_slot.shape[0]
    slots = cold_row.shape[1] * cold_row.shape[2]
    per_peer = cold_row.shape[2]
    rounded = table.astype(jnp.bfloat16)
    hot_full = lax.all_gather(table[hot_slot], ("rows", "grp"), axis=0, tiled=True)
    hot_copy = hot_full.astype(jnp.bfloat16)
    requests = cold_row[0].reshape(n_rows, n_grp, per_peer)
    arrived = lax.all_to_all(
        lax.all_to_all(requests, "rows", split_axis=0, concat_axis=0, tiled=True),
        "grp",
        split_axis=1,
        concat_axis=1,
        tiled=True,
    )
    looked = rounded[arrived.reshape(-1)].reshape(n_rows, n_grp, per_peer, width)
    returned = lax.all_to_all(
        lax.all_to_all(looked, "rows", split_axis=0, concat_axis=0, tiled=True),
        "grp",
        split_axis=1,
        concat_axis=1,
        tiled=True,
    )
    flat_rows = returned.reshape(slots, width)
    bags = cold_bag[0].reshape(slots)
    selector = jnp.arange(samples, dtype=jnp.int32)[:, None] == bags[None, :]
    cold_pooled = jnp.dot(
        selector.astype(jnp.bfloat16), flat_rows, preferred_element_type=jnp.float32
    )
    hot_pooled = jnp.sum(hot_copy[hot_pick].astype(jnp.float32), axis=1)
    pooled = cold_pooled + hot_pooled
    score = jnp.sum(pooled * dense, axis=1) / width**0.5
    err = jax.nn.sigmoid(score) - label.astype(jnp.float32)
    grad = err[:, None] * dense
    slot_grad = lax.dot_general(
        selector.astype(jnp.float32),
        grad,
        (((0,), (0,)), ((), ())),
        precision=lax.Precision.HIGHEST,
        preferred_element_type=jnp.float32,
    )
    delivered = lax.all_to_all(
        lax.all_to_all(
            slot_grad.reshape(n_rows, n_grp, per_peer, width),
            "rows",
            split_axis=0,
            concat_axis=0,
            tiled=True,
        ),
        "grp",
        split_axis=1,
        concat_axis=1,
        tiled=True,
    )
    table_grad = jax.ops.segment_sum(
        delivered.reshape(slots, width), arrived.reshape(slots), num_segments=table.shape[0]
    )
    hot_total = hot_copy.shape[0]
    spread = jnp.repeat(grad, hot_pick.shape[1], axis=0)
    hot_local = jax.ops.segment_sum(spread, hot_pick.reshape(-1), num_segments=hot_total)
    quarter = lax.psum_scatter(hot_local, "grp", scatter_dimension=0, tiled=True)
    crossed = lax.psum(quarter, "rows")
    summed = lax.all_gather(crossed, "grp", axis=0, tiled=True)
    start = lax.axis_index(("rows", "grp")) * own_hot
    own_grad = lax.dynamic_slice_in_dim(summed, start, own_hot, 0)
    table_grad = table_grad.at[hot_slot].add(own_grad)
    new_table = table - 0.1 * table_grad
    hot_new = hot_full - 0.1 * summed
    return (pooled, new_table, hot_new)


def solution(mesh):
    placed = (
        P(("rows", "grp"), None),
        P(("rows", "grp")),
        P(("rows", "grp"), None, None),
        P(("rows", "grp"), None, None),
        P(("rows", "grp"), None),
        P(("rows", "grp"), None),
        P(("rows", "grp")),
    )
    return jax.shard_map(
        body,
        mesh=mesh,
        in_specs=placed,
        out_specs=(P(("rows", "grp"), None), P(("rows", "grp"), None), P()),
        check_vma=False,
    )
```

profile of v0, /device:TPU:0, one launch (start us, length us, event | category | flops | bytes accessed | tf_op | source)
XLA Modules:
  0.0 316.5 jit_solution(10149955036070640280)
XLA Ops:
  7.2 0.8 reshape.122
  8.0 13.6 %all_to_all.30 = s32[8,1,256]{2,1,0:T(1,128)S(1)} all-to-all(s32[8,1,256]{2,1,0:T(1,128)S(1)} %reshape.122), channel_id=1, replica_groups=mesh['rows'=8,'grp'=4] {'rows'}, dimensions={0} | all-to-all | bytes 16384 | tf_op jit(solution)/shard_map/all_to_all | solution.py:20
  22.9 0.7 reshape.124
  23.5 3.2 %all-to-all-start.1 = ((s32[4,1,512]{2,1,0:T(1,128)}), s32[4,1,512]{2,1,0:T(1,128)S(1)}, u32[]{:S(2)}, u32[]{:S(2)}) async-start(s32[4,1,512]{2,1,0:T(1,128)} %reshape.124), calls=%async_computation.1 | async-start | bytes 16384 | tf_op jit(solution)/shard_map/all_to_all | solution.py:19
  26.8 1.7 convert_element_type.14
  28.5 2.1 all-to-all-done.1
  31.5 9.1 %gather_fusion = bf16[2048,256]{1,0:T(8,128)(2,1)} fusion(bf16[2048,256]{1,0:T(8,128)(2,1)S(1)} %convert_element_type.14, s32[2048]{0:T(1024)S(1)} %broadcast_clamp_fusion.1), kind=kCustom, calls=%fused_computation | custom fusion | bytes 2105344 | tf_op jit(solution)/shard_map/gather | solution.py:26
  40.5 4.4 %all-to-all-start.2 = ((bf16[8,4,64,256]{3,2,1,0:T(8,128)(2,1)}), bf16[8,4,64,256]{3,2,1,0:T(8,128)(2,1)}, u32[]{:S(2)}, u32[]{:S(2)}) async-start(bf16[8,4,64,256]{3,2,1,0:T(8,128)(2,1)} %bitcast.19), calls=%async_computation.2 | async-start | bytes 2097152 | tf_op jit(solution)/shard_map/all_to_all | solution.py:28
  44.9 0.8 copy.42
  46.4 24.6 %all-to-all-done.2 = bf16[8,4,64,256]{3,2,1,0:T(8,128)(2,1)} async-done(((bf16[8,4,64,256]{3,2,1,0:T(8,128)(2,1)}), bf16[8,4,64,256]{3,2,1,0:T(8,128)(2,1)}, u32[]{:S(2)}, u32[]{:S(2)}) %all-to-all-start.2) | async-done | bytes 1048608 | tf_op jit(solution)/shard_map/all_to_all | solution.py:28
  70.9 2.3 copy.37
  73.2 4.4 %all-to-all-start.3 = ((bf16[8,4,64,256]{3,2,0,1:T(8,128)(2,1)}), bf16[8,4,64,256]{3,2,0,1:T(8,128)(2,1)}, u32[]{:S(2)}, u32[]{:S(2)}) async-start(bf16[8,4,64,256]{3,2,0,1:T(8,128)(2,1)} %copy.37), calls=%async_computation.3 | async-start | bytes 2097152 | tf_op jit(solution)/shard_map/all_to_all | solution.py:27
  77.6 46.8 %all-gather = f32[512,256]{1,0:T(8,128)S(1)} all-gather(f32[16,256]{1,0:T(8,128)S(1)} %gather_fusion.1), channel_id=2, replica_groups=mesh['rows'=8,'grp'=4] {'rows','grp'}, dimensions={0}, use_global_device_ids=true | all-gather | bytes 540672 | tf_op jit(solution)/shard_map/all_gather | solution.py:16
  124.8 9.1 %gather_fusion.2 = bf16[2048,256]{1,0:T(8,128)(2,1)} fusion(bf16[512,256]{1,0:T(8,128)(2,1)S(1)} %convert_element_type.15, s32[2048]{0:T(1024)S(1)} %broadcast_clamp_fusion), kind=kCustom, calls=%fused_computation.2 | custom fusion | bytes 2105344 | tf_op jit(solution)/shard_map/gather | solution.py:40
  133.8 1.9 convert_reduce_fusion
  135.7 0.8 copy.40
  136.7 1.3 copy.38
  138.0 1.7 multiply_reduce_fusion
  139.8 3.2 fusion.2
  142.9 4.3 %all-to-all-start.4 = ((f32[8,4,64,256]{3,2,1,0:T(8,128)}), f32[8,4,64,256]{3,2,1,0:T(8,128)}, u32[]{:S(2)}, u32[]{:S(2)}) async-start(f32[8,4,64,256]{3,2,1,0:T(8,128)} %bitcast.18), calls=%async_computation.4 | async-start | bytes 4194304 | tf_op jit(solution)/shard_map/all_to_all | solution.py:53
  147.6 12.4 %scatter_custom_fusion.1 = f32[512,256]{1,0:T(8,128)} fusion(s32[2048]{0:T(1024)S(1)} %reshape.94, f32[256,256]{1,0:T(8,128)S(1)} %broadcast_multiply_fusion, f32[]{:T(128)} %constant.15.clone.1), kind=kCustom, calls=%fused_computation.7 | custom fusion | flops 524288 | bytes 786436 | tf_op jit(solution)/shard_map/scatter-add | solution.py:70
  160.0 36.3 %all-to-all-done.4 = f32[8,4,64,256]{3,2,1,0:T(8,128)} async-done(((f32[8,4,64,256]{3,2,1,0:T(8,128)}), f32[8,4,64,256]{3,2,1,0:T(8,128)}, u32[]{:S(2)}, u32[]{:S(2)}) %all-to-all-start.4) | async-done | bytes 2097184 | tf_op jit(solution)/shard_map/all_to_all | solution.py:53
  196.3 3.1 copy.43
  199.4 4.4 %all-to-all-start.5 = ((f32[8,4,64,256]{3,2,0,1:T(8,128)}), f32[8,4,64,256]{3,2,0,1:T(8,128)}, u32[]{:S(2)}, u32[]{:S(2)}) async-start(f32[8,4,64,256]{3,2,0,1:T(8,128)} %copy.43), calls=%async_computation.5 | async-start | bytes 4194304 | tf_op jit(solution)/shard_map/all_to_all | solution.py:52
  204.7 0.8 copy.46
  205.6 72.4 %all-reduce.2.cloned.1.call-done = f32[128,256]{1,0:T(8,128)} async-done(((f32[128,256]{1,0:T(8,128)}), f32[128,256]{1,0:T(8,128)}) %all-reduce.2.cloned.1.call-update) | async-done | bytes 131088 | tf_op jit(solution)/shard_map/psum | solution.py:72
  278.0 7.5 %all_gather.7 = f32[512,256]{1,0:T(8,128)S(1)} all-gather(f32[128,256]{1,0:T(8,128)} %all-reduce.2.cloned.1.call-done), channel_id=1, replica_groups=mesh['rows'=8,'grp'=4] {'grp'}, dimensions={0}, use_global_device_ids=true | all-gather | bytes 655360 | tf_op jit(solution)/shard_map/all_gather | solution.py:73
  285.5 0.9 multiply_subtract_fusion.1
  286.4 3.1 copy.44
  289.5 13.4 %scatter_custom_fusion = f32[2048,256]{1,0:T(8,128)} fusion(s32[2048]{0:T(1024)S(1)} %reshape.86, f32[2048,256]{1,0:T(8,128)} %bitcast.20, f32[]{:T(128)} %constant.15.clone.1), kind=kCustom, calls=%fused_computation.15 | custom fusion | flops 524288 | bytes 2097664 | tf_op jit(solution)/shard_map/scatter-add | solution.py:65
  302.9 3.6 %scatter_custom_fusion.2 = f32[2048,256]{1,0:T(8,128)} fusion(f32[2048,256]{1,0:T(8,128)} %scatter_custom_fusion, s32[16]{0:T(128)S(1)} %compare_select_fusion.2, f32[512,256]{1,0:T(8,128)S(1)} %all_gather.7, s32[]{:T(128)S(6)} %select_n.23, s32[]{:T(128)} %constant.12.clone.1), kind=kCustom, calls=%fused_computation.25 | custom fusion | flops 4096 | bytes 2114052 | tf_op jit(solution)/shard_map/scatter-add | solution.py:76
  306.5 3.2 %multiply_subtract_fusion = f32[2048,256]{1,0:T(8,128)} fusion(f32[2048,256]{1,0:T(8,128)S(1)} %copy-done, f32[2048,256]{1,0:T(8,128)} %scatter_custom_fusion.2), kind=kLoop, calls=%fused_computation.9 | loop fusion | flops 1048576 | bytes 6291456 | tf_op jit(solution)/shard_map/sub | solution.py:77
  (45 shorter events, 4.3 us)
Async XLA Ops:
  23.5 7.0 %all-to-all-start.1 = ((s32[4,1,512]{2,1,0:T(1,128)}), s32[4,1,512]{2,1,0:T(1,128)S(1)}, u32[]{:S(2)}, u32[]{:S(2)}) async-start(s32[4,1,512]{2,1,0:T(1,128)} %reshape.124), calls=%async_computation.1 | async-start | bytes 16384 | tf_op jit(solution)/shard_map/all_to_all | solution.py:19
  31.5 13.5 %copy-start.1 = (f32[256,256]{1,0:T(8,128)S(1)}, f32[256,256]{1,0:T(8,128)}, u32[]{:S(2)}) copy-start(f32[256,256]{1,0:T(8,128)} %param.12) | copy-start | bytes 786436
  40.5 5.2 %copy-start.6 = (s32[16]{0:T(128)S(1)}, s32[16]{0:T(128)}, u32[]{:S(2)}) copy-start(s32[16]{0:T(128)} %param.8) | copy-start | bytes 196
  40.5 5.2 %copy-start = (f32[2048,256]{1,0:T(8,128)S(1)}, f32[2048,256]{1,0:T(8,128)}, u32[]{:S(2)}) copy-start(f32[2048,256]{1,0:T(8,128)} %param.7) | copy-start | bytes 6291460
  40.5 30.4 %all-to-all-start.2 = ((bf16[8,4,64,256]{3,2,1,0:T(8,128)(2,1)}), bf16[8,4,64,256]{3,2,1,0:T(8,128)(2,1)}, u32[]{:S(2)}, u32[]{:S(2)}) async-start(bf16[8,4,64,256]{3,2,1,0:T(8,128)(2,1)} %bitcast.19), calls=%async_computation.2 | async-start | bytes 2097152 | tf_op jit(solution)/shard_map/all_to_all | solution.py:28
  73.2 51.2 %copy-start.3 = (s32[256,8]{0,1:T(8,128)S(1)}, s32[256,8]{0,1:T(8,128)}, u32[]{:S(2)}) copy-start(s32[256,8]{0,1:T(8,128)} %param.11) | copy-start | bytes 24580
  73.2 63.4 %all-to-all-start.3 = ((bf16[8,4,64,256]{3,2,0,1:T(8,128)(2,1)}), bf16[8,4,64,256]{3,2,0,1:T(8,128)(2,1)}, u32[]{:S(2)}, u32[]{:S(2)}) async-start(bf16[8,4,64,256]{3,2,0,1:T(8,128)(2,1)} %copy.37), calls=%async_computation.3 | async-start | bytes 2097152 | tf_op jit(solution)/shard_map/all_to_all | solution.py:27
  124.7 11.8 %copy-start.4 = (s32[1,32,64]{2,1,0:T(8,128)S(1)}, s32[1,32,64]{2,1,0:T(8,128)}, u32[]{:S(2)}) copy-start(s32[1,32,64]{2,1,0:T(8,128)} %param.10) | copy-start | bytes 24580
  136.6 1.4 copy-start.2
  136.7 3.0 copy-start.5
  142.9 53.4 %all-to-all-start.4 = ((f32[8,4,64,256]{3,2,1,0:T(8,128)}), f32[8,4,64,256]{3,2,1,0:T(8,128)}, u32[]{:S(2)}, u32[]{:S(2)}) async-start(f32[8,4,64,256]{3,2,1,0:T(8,128)} %bitcast.18), calls=%async_computation.4 | async-start | bytes 4194304 | tf_op jit(solution)/shard_map/all_to_all | solution.py:53
  147.3 56.7 %reduce-scatter.2.cloned.1.call-start = ((), (), s32[]{:S(2)}) async-start(), calls=%async_computation.7 | async-start | bytes 655360 | tf_op jit(solution)/shard_map/reduce_scatter | solution.py:71
  199.4 86.9 %all-to-all-start.5 = ((f32[8,4,64,256]{3,2,0,1:T(8,128)}), f32[8,4,64,256]{3,2,0,1:T(8,128)}, u32[]{:S(2)}, u32[]{:S(2)}) async-start(f32[8,4,64,256]{3,2,0,1:T(8,128)} %copy.43), calls=%async_computation.5 | async-start | bytes 4194304 | tf_op jit(solution)/shard_map/all_to_all | solution.py:52
  203.9 74.1 %all-reduce.2.cloned.1.call-start = ((), (), s32[]{:S(2)}) async-start(), calls=%async_computation.8 | async-start | bytes 262144 | tf_op jit(solution)/shard_map/psum | solution.py:72
Sparse Core Ops, SparseCore 0:
  160.1 21.9 reduce-scatter.1
  208.1 69.8 all-reduce.1
where the time goes:
time: 317 us; the launch traced here: 316 us
  waiting for transfers between devices  136 us (43%)
  blocking collectives  67.9 us (21%)
  other arithmetic  38.5 us (12%)
  local copies, waits for them, and re-layouts  34 us (11%)
  starting transfers between devices  20.9 us (7%)
  between operations  14.3 us (5%)
  matrix products  4.82 us (2%)
    psum x1, waiting for transfers between devices, body(): crossed = lax.psum(quarter, 'rows')  72.4 us
    all_gather x1, blocking collectives, body(): lax.all_gather(table[hot_slot], ('rows', 'grp'), axis=0, tiled=True)  46.8 us
    all_to_all x1, waiting for transfers between devices, body(): lax.all_to_all(slot_grad.reshape(n_rows, n_grp, per_peer, width), 'rows',...  36.3 us
    all_to_all x1, waiting for transfers between devices, body(): lax.all_to_all(looked, 'rows', split_axis=0, concat_axis=0, tiled=True)  24.6 us
    all_to_all x1, blocking collectives, body(): lax.all_to_all(requests, 'rows', split_axis=0, concat_axis=0, tiled=True)  13.6 us
    scatter-add x1, other arithmetic, body(): jax.ops.segment_sum(delivered.reshape(slots, width), arrived.reshape(slot...  13.4 us
    scatter-add x1, other arithmetic, body(): jax.ops.segment_sum(spread, hot_pick.reshape(-1), num_segments=hot_total)  12.4 us
    gather x1, local copies, waits for them, and re-layouts, body(): rounded[arrived.reshape(-1)].reshape(n_rows, n_grp, per_peer, width)  9.06 us
  transfers between devices with their start and end apart: 7, of which 4 were waited for; matrix products, arithmetic and copies ran while one was open for 10% of the time, Pallas kernels for 0%

commit v1 on v0

--- a/solution.py
+++ b/solution.py
@@ -69,7 +69,7 @@
     spread = jnp.repeat(grad, hot_pick.shape[1], axis=0)
     hot_local = jax.ops.segment_sum(spread, hot_pick.reshape(-1), num_segments=hot_total)
     quarter = lax.psum_scatter(hot_local, "grp", scatter_dimension=0, tiled=True)
-    crossed = lax.psum(quarter, "rows")
+    crossed = jnp.sum(lax.all_gather(quarter, "rows"), axis=0)
     summed = lax.all_gather(crossed, "grp", axis=0, tiled=True)
     start = lax.axis_index(("rows", "grp")) * own_hot
     own_grad = lax.dynamic_slice_in_dim(summed, start, own_hot, 0)

time: 317 us -> 266 us (0.84)
  waiting for transfers between devices: 136 us -> 82.7 us
    psum x1 -> x0, waiting for transfers between devices: 72.4 us -> none  [body(): crossed = lax.psum(quarter, 'rows')]
    reduce_scatter x1, waiting for transfers between devices: 0.02 us -> 22.1 us  [body(): lax.psum_scatter(hot_local, 'grp', scatter_dimension=0, tiled=True)]
    all_to_all x1, waiting for transfers between devices: 36.3 us -> 14.7 us  [body(): lax.all_to_all(slot_grad.reshape(n_rows, n_grp, per_peer, width), 'rows',...]
    all_gather x0 -> x1, waiting for transfers between devices: none -> 19.2 us  [body(): crossed = jnp.sum(lax.all_gather(quarter, 'rows'), axis=0)]
  transfers between devices with their start and end apart: 7 -> 7, of which waited for: 4 -> 5; matrix products, arithmetic and copies ran while one was open for 10% -> 13% of each run, Pallas kernels for 0% -> 0%
where the time goes in v1:
time: 266 us; the launch traced here: 265 us
  waiting for transfers between devices  82.7 us (31%)
  blocking collectives  68.2 us (26%)
  other arithmetic  39.8 us (15%)
  local copies, waits for them, and re-layouts  34 us (13%)
  starting transfers between devices  20.9 us (8%)
  between operations  14.3 us (5%)
  matrix products  4.82 us (2%)
    all_gather x1, blocking collectives, body(): lax.all_gather(table[hot_slot], ('rows', 'grp'), axis=0, tiled=True)  46.8 us
    all_to_all x1, waiting for transfers between devices, body(): lax.all_to_all(looked, 'rows', split_axis=0, concat_axis=0, tiled=True)  24.6 us
    reduce_scatter x1, waiting for transfers between devices, body(): lax.psum_scatter(hot_local, 'grp', scatter_dimension=0, tiled=True)  22.1 us
    all_gather x1, waiting for transfers between devices, body(): crossed = jnp.sum(lax.all_gather(quarter, 'rows'), axis=0)  19.2 us
    all_to_all x1, waiting for transfers between devices, body(): lax.all_to_all(slot_grad.reshape(n_rows, n_grp, per_peer, width), 'rows',...  14.7 us
    all_to_all x1, blocking collectives, body(): lax.all_to_all(requests, 'rows', split_axis=0, concat_axis=0, tiled=True)  13.6 us
    scatter-add x1, other arithmetic, body(): jax.ops.segment_sum(delivered.reshape(slots, width), arrived.reshape(slot...  13.4 us
    scatter-add x1, other arithmetic, body(): jax.ops.segment_sum(spread, hot_pick.reshape(-1), num_segments=hot_total)  12.4 us
  transfers between devices with their start and end apart: 7, of which 5 were waited for; matrix products, arithmetic and copies ran while one was open for 13% of the time, Pallas kernels for 0%

profile of v1, /device:TPU:0, one launch (start us, length us, event | category | flops | bytes accessed | tf_op | source)
XLA Modules:
  0.0 264.7 jit_solution(10905864563783044367)
XLA Ops:
  8.0 13.6 %all_to_all.30 = s32[8,1,256]{2,1,0:T(1,128)S(1)} all-to-all(s32[8,1,256]{2,1,0:T(1,128)S(1)} %reshape.123), channel_id=1, replica_groups=mesh['rows'=8,'grp'=4] {'rows'}, dimensions={0} | all-to-all | bytes 16384 | tf_op jit(solution)/shard_map/all_to_all | solution.py:20
  23.5 3.2 %all-to-all-start.1 = ((s32[4,1,512]{2,1,0:T(1,128)}), s32[4,1,512]{2,1,0:T(1,128)S(1)}, u32[]{:S(2)}, u32[]{:S(2)}) async-start(s32[4,1,512]{2,1,0:T(1,128)} %reshape.125), calls=%async_computation.1 | async-start | bytes 16384 | tf_op jit(solution)/shard_map/all_to_all | solution.py:19
  26.8 1.7 convert_element_type.14
  28.5 2.1 all-to-all-done.1
  31.5 9.1 %gather_fusion = bf16[2048,256]{1,0:T(8,128)(2,1)} fusion(bf16[2048,256]{1,0:T(8,128)(2,1)S(1)} %convert_element_type.14, s32[2048]{0:T(1024)S(1)} %broadcast_clamp_fusion.1), kind=kCustom, calls=%fused_computation | custom fusion | bytes 2105344 | tf_op jit(solution)/shard_map/gather | solution.py:26
  40.5 4.4 %all-to-all-start.2 = ((bf16[8,4,64,256]{3,2,1,0:T(8,128)(2,1)}), bf16[8,4,64,256]{3,2,1,0:T(8,128)(2,1)}, u32[]{:S(2)}, u32[]{:S(2)}) async-start(bf16[8,4,64,256]{3,2,1,0:T(8,128)(2,1)} %bitcast.20), calls=%async_computation.2 | async-start | bytes 2097152 | tf_op jit(solution)/shard_map/all_to_all | solution.py:28
  44.9 0.8 copy.54
  46.4 24.6 %all-to-all-done.2 = bf16[8,4,64,256]{3,2,1,0:T(8,128)(2,1)} async-done(((bf16[8,4,64,256]{3,2,1,0:T(8,128)(2,1)}), bf16[8,4,64,256]{3,2,1,0:T(8,128)(2,1)}, u32[]{:S(2)}, u32[]{:S(2)}) %all-to-all-start.2) | async-done | bytes 1048608 | tf_op jit(solution)/shard_map/all_to_all | solution.py:28
  70.9 2.3 copy.49
  73.2 4.4 %all-to-all-start.3 = ((bf16[8,4,64,256]{3,2,0,1:T(8,128)(2,1)}), bf16[8,4,64,256]{3,2,0,1:T(8,128)(2,1)}, u32[]{:S(2)}, u32[]{:S(2)}) async-start(bf16[8,4,64,256]{3,2,0,1:T(8,128)(2,1)} %copy.49), calls=%async_computation.3 | async-start | bytes 2097152 | tf_op jit(solution)/shard_map/all_to_all | solution.py:27
  77.6 46.8 %all-gather = f32[512,256]{1,0:T(8,128)S(1)} all-gather(f32[16,256]{1,0:T(8,128)S(1)} %gather_fusion.1), channel_id=2, replica_groups=mesh['rows'=8,'grp'=4] {'rows','grp'}, dimensions={0}, use_global_device_ids=true | all-gather | bytes 540672 | tf_op jit(solution)/shard_map/all_gather | solution.py:16
  124.8 9.1 %gather_fusion.2 = bf16[2048,256]{1,0:T(8,128)(2,1)} fusion(bf16[512,256]{1,0:T(8,128)(2,1)S(1)} %convert_element_type.15, s32[2048]{0:T(1024)S(1)} %broadcast_clamp_fusion), kind=kCustom, calls=%fused_computation.2 | custom fusion | bytes 2105344 | tf_op jit(solution)/shard_map/gather | solution.py:40
  133.8 1.9 convert_reduce_fusion
  135.7 0.8 copy.52
  136.7 1.3 copy.50
  138.0 1.7 multiply_reduce_fusion
  139.8 3.2 %fusion.2 = f32[2048,256]{1,0:T(8,128)} fusion(f32[256,256]{1,0:T(8,128)S(1)} %broadcast_multiply_fusion, s32[2048]{0:T(1024)S(1)} %eq.16), kind=kOutput, calls=%fused_computation.11 | convolution fusion | flops 1611137024 | bytes 2367488 | tf_op jit(solution)/shard_map/dot_general | solution.py:45
  142.9 4.3 %all-to-all-start.4 = ((f32[8,4,64,256]{3,2,1,0:T(8,128)}), f32[8,4,64,256]{3,2,1,0:T(8,128)}, u32[]{:S(2)}, u32[]{:S(2)}) async-start(f32[8,4,64,256]{3,2,1,0:T(8,128)} %bitcast.19), calls=%async_computation.4 | async-start | bytes 4194304 | tf_op jit(solution)/shard_map/all_to_all | solution.py:53
  147.6 12.4 %scatter_custom_fusion.1 = f32[512,256]{1,0:T(8,128)} fusion(s32[2048]{0:T(1024)S(1)} %reshape.94, f32[256,256]{1,0:T(8,128)S(1)} %broadcast_multiply_fusion, f32[]{:T(128)} %constant.15.clone.1), kind=kCustom, calls=%fused_computation.7 | custom fusion | flops 524288 | bytes 786436 | tf_op jit(solution)/shard_map/scatter-add | solution.py:70
  160.0 22.1 %reduce-scatter.2.cloned.1.call-done = f32[128,256]{1,0:T(8,128)} async-done(((f32[512,256]{1,0:T(8,128)}), f32[128,256]{1,0:T(8,128)}) %reduce-scatter.2.cloned.1.call-update) | async-done | bytes 131088 | tf_op jit(solution)/shard_map/reduce_scatter | solution.py:71
  182.2 14.7 %all-to-all-done.4 = f32[8,4,64,256]{3,2,1,0:T(8,128)} async-done(((f32[8,4,64,256]{3,2,1,0:T(8,128)}), f32[8,4,64,256]{3,2,1,0:T(8,128)}, u32[]{:S(2)}, u32[]{:S(2)}) %all-to-all-start.4) | async-done | bytes 2097184 | tf_op jit(solution)/shard_map/all_to_all | solution.py:53
  196.8 3.1 %copy.55 = f32[8,4,64,256]{3,2,0,1:T(8,128)} copy(f32[8,4,64,256]{3,2,1,0:T(8,128)} %all-to-all-done.4) | data formatting | bytes 4194304 | tf_op jit(solution)/shard_map/all_to_all | solution.py:53
  200.0 4.4 %all-to-all-start.5 = ((f32[8,4,64,256]{3,2,0,1:T(8,128)}), f32[8,4,64,256]{3,2,0,1:T(8,128)}, u32[]{:S(2)}, u32[]{:S(2)}) async-start(f32[8,4,64,256]{3,2,0,1:T(8,128)} %copy.55), calls=%async_computation.5 | async-start | bytes 4194304 | tf_op jit(solution)/shard_map/all_to_all | solution.py:52
  204.5 0.8 copy.58
  205.4 19.2 %all-gather.4.cloned.1.call-done = f32[1024,256]{1,0:T(8,128)} async-done(((f32[128,256]{1,0:T(8,128)}), f32[1024,256]{1,0:T(8,128)}) %all-gather.4.cloned.1.call-update) | async-done | bytes 1048592 | tf_op jit(solution)/shard_map/all_gather | solution.py:72
  224.6 1.3 reduce_sum.29
  225.9 7.8 %all_gather.15 = f32[512,256]{1,0:T(8,128)S(1)} all-gather(f32[128,256]{1,0:T(8,128)S(1)} %reduce_sum.29), channel_id=1, replica_groups=mesh['rows'=8,'grp'=4] {'grp'}, dimensions={0}, use_global_device_ids=true | all-gather | bytes 655360 | tf_op jit(solution)/shard_map/all_gather | solution.py:73
  233.7 0.9 multiply_subtract_fusion.1
  234.6 3.1 %copy.56 = f32[8,4,64,256]{3,2,1,0:T(8,128)} copy(f32[8,4,64,256]{3,2,0,1:T(8,128)} %all-to-all-done.5) | data formatting | bytes 4194304 | tf_op jit(solution)/shard_map/all_to_all | solution.py:52
  237.7 13.4 %scatter_custom_fusion = f32[2048,256]{1,0:T(8,128)} fusion(s32[2048]{0:T(1024)S(1)} %reshape.86, f32[2048,256]{1,0:T(8,128)} %bitcast.21, f32[]{:T(128)} %constant.15.clone.1), kind=kCustom, calls=%fused_computation.15 | custom fusion | flops 524288 | bytes 2097664 | tf_op jit(solution)/shard_map/scatter-add | solution.py:65
  251.1 3.6 %scatter_custom_fusion.2 = f32[2048,256]{1,0:T(8,128)} fusion(f32[2048,256]{1,0:T(8,128)} %scatter_custom_fusion, s32[16]{0:T(128)S(1)} %compare_select_fusion.2, f32[512,256]{1,0:T(8,128)S(1)} %all_gather.15, s32[]{:T(128)S(6)} %select_n.23, s32[]{:T(128)} %constant.12.clone.1), kind=kCustom, calls=%fused_computation.25 | custom fusion | flops 4096 | bytes 2114052 | tf_op jit(solution)/shard_map/scatter-add | solution.py:76
  254.7 3.2 %multiply_subtract_fusion = f32[2048,256]{1,0:T(8,128)} fusion(f32[2048,256]{1,0:T(8,128)S(1)} %copy-done, f32[2048,256]{1,0:T(8,128)} %scatter_custom_fusion.2), kind=kLoop, calls=%fused_computation.9 | loop fusion | flops 1048576 | bytes 6291456 | tf_op jit(solution)/shard_map/sub | solution.py:77
  (46 shorter events, 5.1 us)
Async XLA Ops:
  23.5 7.0 %all-to-all-start.1 = ((s32[4,1,512]{2,1,0:T(1,128)}), s32[4,1,512]{2,1,0:T(1,128)S(1)}, u32[]{:S(2)}, u32[]{:S(2)}) async-start(s32[4,1,512]{2,1,0:T(1,128)} %reshape.125), calls=%async_computation.1 | async-start | bytes 16384 | tf_op jit(solution)/shard_map/all_to_all | solution.py:19
  31.5 13.5 %copy-start.1 = (f32[256,256]{1,0:T(8,128)S(1)}, f32[256,256]{1,0:T(8,128)}, u32[]{:S(2)}) copy-start(f32[256,256]{1,0:T(8,128)} %param.12) | copy-start | bytes 786436
  40.5 5.2 %copy-start.6 = (s32[16]{0:T(128)S(1)}, s32[16]{0:T(128)}, u32[]{:S(2)}) copy-start(s32[16]{0:T(128)} %param.8) | copy-start | bytes 196
  40.5 5.2 %copy-start = (f32[2048,256]{1,0:T(8,128)S(1)}, f32[2048,256]{1,0:T(8,128)}, u32[]{:S(2)}) copy-start(f32[2048,256]{1,0:T(8,128)} %param.7) | copy-start | bytes 6291460
  40.5 30.4 %all-to-all-start.2 = ((bf16[8,4,64,256]{3,2,1,0:T(8,128)(2,1)}), bf16[8,4,64,256]{3,2,1,0:T(8,128)(2,1)}, u32[]{:S(2)}, u32[]{:S(2)}) async-start(bf16[8,4,64,256]{3,2,1,0:T(8,128)(2,1)} %bitcast.20), calls=%async_computation.2 | async-start | bytes 2097152 | tf_op jit(solution)/shard_map/all_to_all | solution.py:28
  73.2 51.2 %copy-start.3 = (s32[256,8]{0,1:T(8,128)S(1)}, s32[256,8]{0,1:T(8,128)}, u32[]{:S(2)}) copy-start(s32[256,8]{0,1:T(8,128)} %param.11) | copy-start | bytes 24580
  73.2 63.4 %all-to-all-start.3 = ((bf16[8,4,64,256]{3,2,0,1:T(8,128)(2,1)}), bf16[8,4,64,256]{3,2,0,1:T(8,128)(2,1)}, u32[]{:S(2)}, u32[]{:S(2)}) async-start(bf16[8,4,64,256]{3,2,0,1:T(8,128)(2,1)} %copy.49), calls=%async_computation.3 | async-start | bytes 2097152 | tf_op jit(solution)/shard_map/all_to_all | solution.py:27
  124.7 11.8 %copy-start.4 = (s32[1,32,64]{2,1,0:T(8,128)S(1)}, s32[1,32,64]{2,1,0:T(8,128)}, u32[]{:S(2)}) copy-start(s32[1,32,64]{2,1,0:T(8,128)} %param.10) | copy-start | bytes 24580
  136.6 1.4 copy-start.2
  136.7 3.0 %copy-start.5 = (s32[256]{0:T(256)S(1)}, s32[256]{0:T(256)}, u32[]{:S(2)}) copy-start(s32[256]{0:T(256)} %param.13) | copy-start | bytes 3076
  142.9 53.9 %all-to-all-start.4 = ((f32[8,4,64,256]{3,2,1,0:T(8,128)}), f32[8,4,64,256]{3,2,1,0:T(8,128)}, u32[]{:S(2)}, u32[]{:S(2)}) async-start(f32[8,4,64,256]{3,2,1,0:T(8,128)} %bitcast.19), calls=%async_computation.4 | async-start | bytes 4194304 | tf_op jit(solution)/shard_map/all_to_all | solution.py:53
  147.3 34.9 %reduce-scatter.2.cloned.1.call-start = ((), (), s32[]{:S(2)}) async-start(), calls=%async_computation.7 | async-start | bytes 655360 | tf_op jit(solution)/shard_map/reduce_scatter | solution.py:71
  160.0 64.6 %all-gather.4.cloned.1.call-start = ((), (), s32[]{:S(2)}) async-start(), calls=%async_computation.8 | async-start | bytes 1179648 | tf_op jit(solution)/shard_map/all_gather | solution.py:72
  200.0 34.6 %all-to-all-start.5 = ((f32[8,4,64,256]{3,2,0,1:T(8,128)}), f32[8,4,64,256]{3,2,0,1:T(8,128)}, u32[]{:S(2)}, u32[]{:S(2)}) async-start(f32[8,4,64,256]{3,2,0,1:T(8,128)} %copy.55), calls=%async_computation.5 | async-start | bytes 4194304 | tf_op jit(solution)/shard_map/all_to_all | solution.py:52
Sparse Core Ops, SparseCore 0:
  160.1 21.9 reduce-scatter.1
  184.3 40.2 all-gather.3
